TPU v7x, 32 devices: a whole 2x2x4 slice. The times are simulated.
32 devices in a mesh: ep: 4 (over y, core), fsdp: 8 (over z, x).
Axes of the slice: x: 2, y: 2, z: 4, core: 2. Of those that a mesh axis runs over, the one named last changes fastest.
Arguments:
- master_down: float32 [16, 6400, 4096], P('ep', None, 'fsdp'), may hold values from -0.109375 to 0.109375
- second_down: bfloat16 [16, 6400, 4096], P('ep', None, 'fsdp'), may hold values from -0.0390625 to 0.0390625
- router_weight: float32 [4096, 16], P('fsdp', 'ep'), may hold values from -0.09375 to 0.09375
- router_gain: float32 [4096], P('fsdp'), may hold values from 0.25 to 1.75
Outputs:
- final_down: bfloat16 [16, 6400, 4096], P('ep', 'fsdp')
- scale_down: float32 [16, 6400], P('ep', 'fsdp')
- serve_router: bfloat16 [4096, 16], replicated
All inputs are finite; a program needn't handle non-finite values.
Results may differ from a plain program's by a relative error of at most 0.001.
Values may be sent and summed in bfloat16 or wider, within the bound.
A program may use at most 256 MiB of HBM per device.

v0:
```python
import functools

import jax
import jax.numpy as jnp
from jax import lax
from jax.experimental import pallas as pl
from jax.experimental.pallas import tpu as pltpu
from jax.sharding import PartitionSpec as P

MESH = pl.DeviceIdType.MESH
LANES = 128
RING = 4
SLOTS = 4


def largest_divisor(size, limit, step):
    return max(d for d in range(step, limit + 1, step) if size % d == 0)


def kernel(dims, master, second, router, gain, final, scales, routers,
           held, narrow, part, gathered, total, inverse, sent, router_part,
           master_sem, second_sem, part_send, part_recv, total_send, total_recv,
           block_send, block_own, block_recv, router_send, router_recv):
    groups, fsdp, experts, steps, rows, width, blocks, size = dims
    chunks = experts * steps
    me, group = lax.axis_index("fsdp"), lax.axis_index("ep")
    peers = [lax.rem(me + k, fsdp) for k in range(1, fsdp)]
    others = [lax.rem(group + k, groups) for k in range(1, groups)]

    def load(t):
        e, s = t // steps, t % steps
        span = pl.ds(pl.multiple_of(s * rows, 8), rows)
        return (
            pltpu.make_async_copy(master.at[e, :, span, :], held.at[t % RING], master_sem.at[t % RING]),
            pltpu.make_async_copy(second.at[e, :, span, :], narrow.at[t % 2], second_sem.at[t % 2]),
        )

    for t in range(min(2, chunks)):
        for copy in load(t):
            copy.start()

    barrier = pltpu.get_barrier_semaphore()
    for p in peers:
        pl.semaphore_signal(barrier, inc=1, device_id={"fsdp": p}, device_id_type=MESH)
    for g in others:
        pl.semaphore_signal(barrier, inc=1, device_id={"ep": g}, device_id_type=MESH)
    pl.semaphore_wait(barrier, len(peers) + len(others))

    def router_copy(p):
        return pltpu.make_async_remote_copy(
            router_part, routers.at[group, me], router_send.at[0], router_recv.at[0],
            device_id={"fsdp": p}, device_id_type=MESH)

    def router_rows(g):
        return pltpu.make_async_remote_copy(
            routers.at[group], routers.at[group], router_send.at[1], router_recv.at[1],
            device_id={"ep": g}, device_id_type=MESH)

    own_router = (router[...] * gain[...]).astype(jnp.bfloat16)
    router_part[...] = own_router
    routers[group, me] = own_router

    def stats(t):
        for copy in load(t):
            copy.wait()
        slot, side = t % RING, t % 2

        def body(d, _):
            for b in range(blocks):
                span = pl.ds(b * size, size)
                x = held[slot, d, span, :] + narrow[side, d, span, :].astype(jnp.float32)
                held[slot, d, span, :] = x
                x = x * x
                acc = x[:, :LANES]
                for c in range(LANES, width, LANES):
                    acc = acc + x[:, c:c + LANES]
                if size < LANES:
                    acc = jnp.concatenate([acc, jnp.zeros((LANES - size, LANES), jnp.float32)], axis=0)
                part[t, d, pl.ds(b, 1), :] = jnp.sum(acc.T, axis=0, keepdims=True)
            return 0

        lax.fori_loop(0, fsdp, body, 0)
        gathered[t, me] = part[t, me]
        for p in peers:
            pltpu.make_async_remote_copy(
                part.at[t, p], gathered.at[t, me], part_send.at[t], part_recv.at[t],
                device_id={"fsdp": p}, device_id_type=MESH).start()

    def many(ref, t, sem):
        seven = ref.at[t, pl.ds(0, fsdp - 1)]
        return pltpu.make_async_copy(seven, seven, sem)

    def reduce(t):
        many(gathered, t, part_recv.at[t]).wait()
        scale = jnp.sqrt(jnp.sum(gathered[t], axis=0))
        scales[t] = scale
        back = 1.0 / scale
        total[t] = back
        inverse[t, me] = back
        for p in peers:
            pltpu.make_async_remote_copy(
                total.at[t], inverse.at[t, me], total_send.at[t], total_recv.at[t],
                device_id={"fsdp": p}, device_id_type=MESH).start()

    def place(t):
        e, s = t // steps, t % steps
        return final.at[e, pl.ds(pl.multiple_of(s * rows, 8), rows), pl.ds(pl.multiple_of(me * width, LANES), width)]

    def own_copy(t):
        return pltpu.make_async_copy(sent.at[t % SLOTS, me], place(t), block_own.at[t % SLOTS])

    def drain(t):
        many(sent, t % SLOTS, block_send.at[t % SLOTS]).wait()
        own_copy(t).wait()

    def norm(t):
        many(inverse, t, total_recv.at[t]).wait()
        many(part, t, part_send.at[t]).wait()
        many(inverse, t, total_send.at[t]).wait()

        @pl.when(t >= SLOTS)
        def _():
            drain(t - SLOTS)

        slot, out = t % RING, t % SLOTS

        def body(d, _):
            for b in range(blocks):
                span = pl.ds(b * size, size)
                row = inverse[t, d, pl.ds(b, 1), :]
                factor = jnp.broadcast_to(row, (LANES, LANES)).T[:size]
                for c in range(0, width, LANES):
                    x = held[slot, d, span, c:c + LANES] * factor
                    sent[out, d, span, c:c + LANES] = x.astype(jnp.bfloat16)
            return 0

        lax.fori_loop(0, fsdp, body, 0)
        for p in peers:
            pltpu.make_async_remote_copy(
                sent.at[out, p], place(t), block_send.at[out], block_recv.at[me],
                device_id={"fsdp": p}, device_id_type=MESH).start()
        own_copy(t).start()

    def step(u, _):
        @pl.when(u < chunks)
        def _():
            stats(u)

        @pl.when((u >= 1) & (u < chunks + 1))
        def _():
            reduce(u - 1)

        @pl.when(u >= 2)
        def _():
            norm(u - 2)

        @pl.when(u + 2 < chunks)
        def _():
            for copy in load(u + 2):
                copy.start()

        return 0

    lax.fori_loop(0, chunks + 2, step, 0)

    for p in peers:
        router_copy(p).start()
    seven = routers.at[group, pl.ds(0, fsdp - 1)]
    pltpu.make_async_copy(seven, seven, router_send.at[0]).wait()
    pltpu.make_async_copy(seven, seven, router_recv.at[0]).wait()
    for g in others:
        router_rows(g).start()
    three = routers.at[pl.ds(0, groups - 1)]
    pltpu.make_async_copy(three, three, router_send.at[1]).wait()
    pltpu.make_async_copy(three, three, router_recv.at[1]).wait()

    def last(t, _):
        drain(t)
        return 0

    lax.fori_loop(max(0, chunks - SLOTS), chunks, last, 0)
    for p in peers:
        column = final.at[:, :, pl.ds(pl.multiple_of(p * width, LANES), width)]
        pltpu.make_async_copy(column, column, block_recv.at[p]).wait()


def solution(mesh):
    groups, fsdp = mesh.shape["ep"], mesh.shape["fsdp"]

    def step(master, second, router, gain):
        experts, height, width = master.shape
        own = height // fsdp
        rows = largest_divisor(own, 160, 8)
        size = largest_divisor(rows, LANES, 8)
        blocks, steps = rows // size, own // rows
        chunks = experts * steps
        dims = (groups, fsdp, experts, steps, rows, width, blocks, size)
        columns = router.shape[1]
        anywhere = pl.BlockSpec(memory_space=pl.ANY)
        inside = pl.BlockSpec(memory_space=pltpu.VMEM)
        tall = (chunks, fsdp, blocks, LANES)
        dma = pltpu.SemaphoreType.DMA
        final, scales, routers = pl.pallas_call(
            functools.partial(kernel, dims),
            out_shape=(
                jax.ShapeDtypeStruct((experts, own, fsdp * width), jnp.bfloat16),
                jax.ShapeDtypeStruct((chunks, blocks, LANES), jnp.float32),
                jax.ShapeDtypeStruct((groups, fsdp, columns, width), jnp.bfloat16),
            ),
            in_specs=[anywhere, anywhere, inside, inside],
            out_specs=(anywhere, inside, inside),
            scratch_shapes=[
                pltpu.VMEM((RING, fsdp, rows, width), jnp.float32),
                pltpu.VMEM((2, fsdp, rows, width), jnp.bfloat16),
                pltpu.VMEM(tall, jnp.float32),
                pltpu.VMEM(tall, jnp.float32),
                pltpu.VMEM((chunks, blocks, LANES), jnp.float32),
                pltpu.VMEM(tall, jnp.float32),
                pltpu.VMEM((SLOTS, fsdp, rows, width), jnp.bfloat16),
                pltpu.VMEM((columns, width), jnp.bfloat16),
                dma((RING,)), dma((2,)),
                dma((chunks,)), dma((chunks,)), dma((chunks,)), dma((chunks,)),
                dma((SLOTS,)), dma((SLOTS,)), dma((fsdp,)),
                dma((2,)), dma((2,)),
            ],
            compiler_params=pltpu.CompilerParams(
                collective_id=0, has_side_effects=True, vmem_limit_bytes=48 * 2**20),
        )(
            master.reshape(experts, fsdp, own, width),
            second.reshape(experts, fsdp, own, width),
            router.T,
            gain[None, :],
        )
        scale = scales[:, :, :size].reshape(experts, own)
        routers = routers.transpose(1, 3, 0, 2).reshape(fsdp * width, groups * columns)
        return final, scale, routers

    return jax.shard_map(
        step,
        mesh=mesh,
        in_specs=(P("ep", None, "fsdp"), P("ep", None, "fsdp"), P("fsdp", "ep"), P("fsdp")),
        out_specs=(P("ep", "fsdp", None), P("ep", "fsdp"), P()),
        check_vma=False,
    )
```

profile of v0, /device:TPU:0, one launch (start us, length us, event | category | flops | bytes accessed | tf_op | source)
XLA Modules:
  0.0 611.6 jit_solution(856490335137560918)
XLA Ops:
  0.6 0.0 copy-start
  0.6 0.7 copy-done
  1.3 0.0 copy-start.1
  1.3 0.7 copy-done.1
  2.0 590.2 %shard_map.67 = (bf16[4,800,4096]{2,1,0:T(8,128)(2,1)}, f32[20,2,128]{2,1,0:T(2,128)S(1)}, bf16[4,8,4,512]{3,2,1,0:T(4,128)(2,1)S(1)}) custom-call(f32[4,8,800,512]{3,2,1,0:T(8,128)} %bitcast.15, bf16[4,8,800,512]{3,2,1,0:T(8,128)(2,1)} %bitcast.16, f32[4,512]{1,0:T(4,128)S(1)} %bitcast.13, f32[1,512]{1,0:T(1,128)S(1)} %bitcast.14), custom_call_target="tpu_custom_call" | custom-call | tf_op jit(solution)/shard_map/pallas_call | solution.py:203
  592.3 0.7 reshape.20
  593.0 0.7 copy.8
  593.7 17.9 %copy.10 = bf16[4,800,4096]{2,1,0:T(8,128)(2,1)} copy(bf16[4,800,4096]{2,1,0:T(8,128)(2,1)} %get-tuple-element.12) | data formatting | bytes 52428800
  (1 shorter events, 0.0 us)
Async XLA Ops:
  0.6 0.7 copy-start
  1.3 0.7 copy-start.1
where the time goes:
time: 612 us
  Pallas kernels  590 us (96%)
  local copies, waits for them, and re-layouts  20.7 us (3%)
    pallas_call x1, Pallas kernels, step(): pl.pallas_call(functools.partial(kernel, dims), out_shape=(jax.ShapeDtype...  590 us
    unnamed x6, local copies, waits for them, and re-layouts  20 us

commit v1 on v0

v1 whole, which is shorter than its diff:
```python
import functools

import jax
import jax.numpy as jnp
from jax import lax
from jax.experimental import pallas as pl
from jax.experimental.pallas import tpu as pltpu
from jax.sharding import PartitionSpec as P

MESH = pl.DeviceIdType.MESH
LANES = 128
AHEAD = 2
SLOTS = 4
FETCH = 3


def largest_divisor(size, limit, step):
    return max(d for d in range(step, limit + 1, step) if size % d == 0)


def exchange(dims, master, second, router, gain, final, scales, routers,
             held, narrow, part, whole, gathered, cross, inverse, sent, router_in, gain_in, router_part,
             master_sem, second_sem, small_sem, whole_send, whole_recv, near_send, near_recv, far_send, far_recv,
             back_send, back_recv, block_send, block_recv, router_send, router_recv):
    groups, fsdp, experts, steps, rows, width, first, ring, wide = dims
    chunks, half = experts * steps, fsdp // 2
    me, group = lax.axis_index("fsdp"), lax.axis_index("ep")
    side, lane = me // half, lax.rem(me, half)
    peers = [lax.rem(me + k, fsdp) for k in range(1, fsdp)]
    near = [lax.rem(lane + k, half) for k in range(1, half)]
    others = [lax.rem(group + k, groups) for k in range(1, groups)]
    partner = lax.rem(me + half, fsdp)

    def load(t):
        e, s = t // steps, lax.rem(t, steps)
        span = pl.ds(pl.multiple_of(s * rows, 8), rows)
        a, b = lax.rem(t, ring), lax.rem(t, wide)
        return (
            pltpu.make_async_copy(master.at[e, :, span, :], held.at[a], master_sem.at[a]),
            pltpu.make_async_copy(second.at[e, :, span, :], narrow.at[b], second_sem.at[b]),
        )

    for t in range(min(FETCH, chunks)):
        for copy in load(t):
            copy.start()
    small = (pltpu.make_async_copy(router, router_in, small_sem.at[0]),
             pltpu.make_async_copy(gain, gain_in, small_sem.at[1]))
    for copy in small:
        copy.start()

    barrier = pltpu.get_barrier_semaphore()
    for p in peers:
        pl.semaphore_signal(barrier, inc=1, device_id={"fsdp": p}, device_id_type=MESH)
    for g in others:
        pl.semaphore_signal(barrier, inc=1, device_id={"ep": g}, device_id_type=MESH)

    def remote(source, target, send, recv, p):
        return pltpu.make_async_remote_copy(
            source, target, send, recv, device_id={"fsdp": p}, device_id_type=MESH)

    def sums(t):
        for copy in load(t):
            copy.wait()
        a, b = lax.rem(t, ring), lax.rem(t, wide)

        def body(j, _):
            for s in range(2):
                d = s * half + j
                x = held[a, d] + narrow[b, d].astype(jnp.float32)
                held[a, d] = x
                x = x * x
                acc = x[:, :LANES]
                for c in range(LANES, width, LANES):
                    acc = acc + x[:, c:c + LANES]
                if rows < LANES:
                    acc = jnp.concatenate([acc, jnp.zeros((LANES - rows, LANES), jnp.float32)], axis=0)
                part[t, j, pl.ds(s, 1), :] = jnp.sum(acc.T, axis=0, keepdims=True)
            return 0

        lax.fori_loop(0, half, body, 0)

        @pl.when(t + FETCH < chunks)
        def _():
            for copy in load(t + FETCH):
                copy.start()

    def send_whole(t):
        whole[t, me] = part[t]
        for p in peers:
            remote(part.at[t], whole.at[t, me], whole_send.at[t], whole_recv.at[t], p).start()

    def send_near(t):
        gathered[t, lane] = part[t, lane]
        for q in near:
            remote(part.at[t, q], gathered.at[t, lane], near_send.at[t], near_recv.at[t], side * half + q).start()

    def many(ref, t, count, sem):
        block = ref.at[t, pl.ds(0, count)]
        return pltpu.make_async_copy(block, block, sem)

    def put_scale(t, scale):
        scales[t] = jnp.where(side == 0, scale[0:1], scale[1:2])

    def send_far(t):
        many(gathered, t, half - 1, near_recv.at[t]).wait()
        cross[t, side] = jnp.sum(gathered[t], axis=0)
        remote(cross.at[t, side], cross.at[t, side], far_send.at[t], far_recv.at[t], partner).start()

    def send_back(t):
        many(cross, t, 1, far_recv.at[t]).wait()
        scale = jnp.sqrt(cross[t, 0] + cross[t, 1])
        put_scale(t, scale)
        inverse[t, lane] = 1.0 / scale
        for q in near:
            remote(inverse.at[t, lane], inverse.at[t, lane], back_send.at[t], back_recv.at[t], side * half + q).start()

    def take_whole(t):
        many(whole, t, fsdp - 1, whole_recv.at[t]).wait()
        total = whole[t, 0]
        for k in range(1, fsdp):
            total = total + whole[t, k]
        scale = jnp.sqrt(total)
        inverse[t] = 1.0 / scale
        gathered[0] = scale
        put_scale(t, gathered[0, lane])
        many(whole, t, fsdp - 1, whole_send.at[t]).wait()

    def take_back(t):
        many(inverse, t, half - 1, back_recv.at[t]).wait()
        many(gathered, t, half - 1, near_send.at[t]).wait()
        many(cross, t, 1, far_send.at[t]).wait()
        many(inverse, t, half - 1, back_send.at[t]).wait()

    def drain(t):
        many(sent, lax.rem(t, SLOTS), fsdp - 1, block_send.at[lax.rem(t, SLOTS)]).wait()

    def norm(t):
        @pl.when(t >= SLOTS)
        def _():
            drain(t - SLOTS)

        e, s = t // steps, lax.rem(t, steps)
        a, out = lax.rem(t, ring), lax.rem(t, SLOTS)
        span = pl.ds(pl.multiple_of(s * rows, 8), rows)
        place = final.at[e, span, pl.ds(pl.multiple_of(me * width, LANES), width)]

        def block(d):
            row = inverse[t, lax.rem(d, half), pl.ds(d // half, 1), :]
            factor = jnp.broadcast_to(row, (LANES, LANES)).T[:rows]
            for c in range(0, width, LANES):
                sent[out, d, :, c:c + LANES] = (held[a, d, :, c:c + LANES] * factor).astype(jnp.bfloat16)

        def push(d):
            remote(sent.at[out, d], place, block_send.at[out], block_recv.at[me], d).start()

        def body(k, _):
            block(lax.rem(me + k, fsdp))

            @pl.when(k > 1)
            def _():
                push(lax.rem(me + k - 1, fsdp))

            return 0

        lax.fori_loop(1, fsdp, body, 0)
        block(me)
        push(lax.rem(me + fsdp - 1, fsdp))
        final[e, span, pl.ds(pl.multiple_of(me * width, LANES), width)] = sent[out, me]

    sums(0)
    pl.semaphore_wait(barrier, len(peers) + len(others))

    def start(t, _):
        @pl.when(t > 0)
        def _():
            sums(t)

        send_whole(t)
        return 0

    lax.fori_loop(0, first, start, 0)

    def step(u, _):
        @pl.when(u < chunks)
        def _():
            sums(u)
            send_near(u)

        t = u - AHEAD

        @pl.when((t >= first) & (t < chunks))
        def _():
            send_far(t)

        v = u - 2 * AHEAD

        @pl.when((v >= first) & (v < chunks))
        def _():
            send_back(v)

        w = u - 3 * AHEAD

        @pl.when(w < first)
        def _():
            take_whole(w)

        @pl.when(w >= first)
        def _():
            take_back(w)

        norm(w)

        @pl.when(u == first)
        def _():
            for copy in small:
                copy.wait()
            own = (router_in[...] * gain_in[...]).astype(jnp.bfloat16)
            router_part[...] = own
            routers[group, me] = own
            for p in peers:
                remote(router_part, routers.at[group, me], router_send.at[0], router_recv.at[0], p).start()

        return 0

    lax.fori_loop(first, chunks + 3 * AHEAD, step, 0)

    seven = routers.at[group, pl.ds(0, fsdp - 1)]
    pltpu.make_async_copy(seven, seven, router_send.at[0]).wait()
    pltpu.make_async_copy(seven, seven, router_recv.at[0]).wait()
    for g in others:
        pltpu.make_async_remote_copy(
            routers.at[group], routers.at[group], router_send.at[1], router_recv.at[1],
            device_id={"ep": g}, device_id_type=MESH).start()
    three = routers.at[pl.ds(0, groups - 1)]
    pltpu.make_async_copy(three, three, router_send.at[1]).wait()
    pltpu.make_async_copy(three, three, router_recv.at[1]).wait()

    def last(t, _):
        drain(t)
        return 0

    lax.fori_loop(max(0, chunks - SLOTS), chunks, last, 0)
    for p in peers:
        column = final.at[:, :, pl.ds(pl.multiple_of(p * width, LANES), width)]
        pltpu.make_async_copy(column, column, block_recv.at[p]).wait()


def write(dims, final_in, scales_in, routers_in, final, scale, router, scale_part, router_part, sems):
    groups, fsdp, experts, steps, rows, width = dims
    columns = routers_in.shape[2]
    big = [pltpu.make_async_copy(final_in.at[e], final.at[e], sems.at[e]) for e in range(experts)]
    for copy in big:
        copy.start()
    for e in range(experts):
        parts = [scales_in[e * steps + s][:, :rows] for s in range(steps)]
        scale_part[e:e + 1, :] = jnp.concatenate(parts, axis=1)
    for g in range(groups):
        for d in range(fsdp):
            router_part[g * columns:(g + 1) * columns, d * width:(d + 1) * width] = routers_in[g, d]
    rest = [pltpu.make_async_copy(scale_part, scale, sems.at[experts]),
            pltpu.make_async_copy(router_part, router, sems.at[experts + 1])]
    for copy in rest:
        copy.start()
    for copy in big + rest:
        copy.wait()


def solution(mesh):
    groups, fsdp = mesh.shape["ep"], mesh.shape["fsdp"]

    def step(master, second, router, gain):
        experts, height, width = master.shape
        own = height // fsdp
        rows = largest_divisor(own, LANES, 8)
        steps = own // rows
        chunks, half = experts * steps, fsdp // 2
        first = min(3 * AHEAD, chunks)
        ring, wide = 3 * AHEAD + FETCH + 1, FETCH + 1
        columns = router.shape[1]
        hbm = pl.BlockSpec(memory_space=pltpu.HBM)
        inside = pl.BlockSpec(memory_space=pltpu.VMEM)
        dma = pltpu.SemaphoreType.DMA
        final, scales, routers = pl.pallas_call(
            functools.partial(exchange, (groups, fsdp, experts, steps, rows, width, first, ring, wide)),
            out_shape=(
                pltpu.VMEM((experts, own, fsdp * width), jnp.bfloat16),
                pltpu.VMEM((chunks, 1, LANES), jnp.float32),
                pltpu.VMEM((groups, fsdp, columns, width), jnp.bfloat16),
            ),
            in_specs=[hbm, hbm, hbm, hbm],
            out_specs=(inside, inside, inside),
            scratch_shapes=[
                pltpu.VMEM((ring, fsdp, rows, width), jnp.float32),
                pltpu.VMEM((wide, fsdp, rows, width), jnp.bfloat16),
                pltpu.VMEM((chunks, half, 2, LANES), jnp.float32),
                pltpu.VMEM((first, fsdp, half, 2, LANES), jnp.float32),
                pltpu.VMEM((chunks, half, 2, LANES), jnp.float32),
                pltpu.VMEM((chunks, 2, 2, LANES), jnp.float32),
                pltpu.VMEM((chunks, half, 2, LANES), jnp.float32),
                pltpu.VMEM((SLOTS, fsdp, rows, width), jnp.bfloat16),
                pltpu.VMEM((columns, width), jnp.float32),
                pltpu.VMEM((1, width), jnp.float32),
                pltpu.VMEM((columns, width), jnp.bfloat16),
                dma((ring,)), dma((wide,)), dma((2,)),
                dma((first,)), dma((first,)),
                dma((chunks,)), dma((chunks,)), dma((chunks,)), dma((chunks,)), dma((chunks,)), dma((chunks,)),
                dma((SLOTS,)), dma((fsdp,)), dma((2,)), dma((2,)),
            ],
            compiler_params=pltpu.CompilerParams(
                collective_id=0, has_side_effects=True, vmem_limit_bytes=28 * 2**20),
        )(
            master.reshape(experts, fsdp, own, width),
            second.reshape(experts, fsdp, own, width),
            pltpu.with_memory_space_constraint(router.T, pltpu.HBM),
            pltpu.with_memory_space_constraint(gain[None, :], pltpu.HBM),
        )
        final, scale, router = pl.pallas_call(
            functools.partial(write, (groups, fsdp, experts, steps, rows, width)),
            out_shape=(
                jax.ShapeDtypeStruct((experts, own, fsdp * width), jnp.bfloat16),
                jax.ShapeDtypeStruct((experts, own), jnp.float32),
                jax.ShapeDtypeStruct((groups * columns, fsdp * width), jnp.bfloat16),
            ),
            in_specs=[inside, inside, inside],
            out_specs=(hbm, hbm, hbm),
            scratch_shapes=[
                pltpu.VMEM((experts, own), jnp.float32),
                pltpu.VMEM((groups * columns, fsdp * width), jnp.bfloat16),
                dma((experts + 2,)),
            ],
            compiler_params=pltpu.CompilerParams(vmem_limit_bytes=2 * 2**20),
        )(final, scales, routers)
        return final, scale, router.T

    return jax.shard_map(
        step,
        mesh=mesh,
        in_specs=(P("ep", None, "fsdp"), P("ep", None, "fsdp"), P("fsdp", "ep"), P("fsdp")),
        out_specs=(P("ep", "fsdp", None), P("ep", "fsdp"), P()),
        check_vma=False,
    )
```

time: 612 us -> 586 us (0.958)
  local copies, waits for them, and re-layouts: 20.7 us -> 0 us
    unnamed x6 -> x0, local copies, waits for them, and re-layouts: 20 us -> none
    pallas_call x1 -> x2, Pallas kernels: 590 us -> 584 us  [the longest x1 575 us: step(): pl.pallas_call(functools.partial(exchange, (groups, fsdp, experts, steps,...]
where the time goes in v1:
time: 586 us; the launch traced here: 584 us
  Pallas kernels  584 us (100%)
    pallas_call x1, Pallas kernels, step(): pl.pallas_call(functools.partial(exchange, (groups, fsdp, experts, steps,...  575 us

profile of v1, /device:TPU:0, one launch (start us, length us, event | category | flops | bytes accessed | tf_op | source)
XLA Modules:
  0.0 584.3 jit_solution(10055176063780580781)
XLA Ops:
  0.6 574.7 %shard_map.67 = (bf16[4,800,4096]{2,1,0:T(8,128)(2,1)S(1)}, f32[40,1,128]{2,1,0:T(1,128)S(1)}, bf16[4,8,4,512]{3,2,1,0:T(4,128)(2,1)S(1)}) custom-call(f32[4,8,800,512]{3,2,1,0:T(8,128)} %bitcast.5, bf16[4,8,800,512]{3,2,1,0:T(8,128)(2,1)} %bitcast.6, f32[4,512]{1,0:T(4,128)} %bitcast.7, f32[1,512]{1,0:T(1,128)} %bitcast.8), custom_call_target="tpu_custom_call" | custom-call | tf_op jit(solution)/shard_map/pallas_call | solution.py:283
  575.4 8.9 %shard_map.68 = (bf16[4,800,4096]{2,1,0:T(8,128)(2,1)}, f32[4,800]{1,0:T(4,128)}, bf16[16,4096]{1,0:T(8,128)(2,1)}) custom-call(bf16[4,800,4096]{2,1,0:T(8,128)(2,1)S(1)} %get-tuple-element.9.final_in, f32[40,1,128]{2,1,0:T(1,128)S(1)} %get-tuple-element.10.scales_in, bf16[4,8,4,512]{3,2,1,0:T(4,128)(2,1)S(1)} %get-tuple-element.11.routers_in), custom_call_target="tpu_custom_call" | custom-call | tf_op jit(solution)/shard_map/pallas_call | solution.py:317

commit v2 on v1

v2 whole, which is shorter than its diff:
```python
import functools

import jax
import jax.numpy as jnp
from jax import lax
from jax.experimental import pallas as pl
from jax.experimental.pallas import tpu as pltpu
from jax.sharding import PartitionSpec as P

MESH = pl.DeviceIdType.MESH
LANES = 128
AHEAD = 2
SLOTS = 4
FETCH = 3
LATE = (5, 3)


def largest_divisor(size, limit, step):
    return max(d for d in range(step, limit + 1, step) if size % d == 0)


def exchange(dims, spans, first, *refs):
    groups, fsdp, steps, rows, width, ring, wide = dims
    if first:
        master, second, router, gain, final, scales, routers, *refs = refs
        router_in, gain_in, router_part, whole, small_sem, whole_send, whole_recv, router_send, router_recv, *refs = refs
    else:
        master, second, _, final, scales, *refs = refs
    (held, narrow, part, gathered, cross, inverse, sent, master_sem, second_sem, near_send, near_recv,
     far_send, far_recv, back_send, back_recv, block_send, block_recv) = refs
    half = fsdp // 2
    me, group = lax.axis_index("fsdp"), lax.axis_index("ep")
    core = lax.rem(group, 2)
    low = jnp.where(core == 0, spans[0][0], spans[1][0])
    chunks = jnp.where(core == 0, spans[0][1], spans[1][1]) - low
    side, lane = me // half, lax.rem(me, half)
    peers = [lax.rem(me + k, fsdp) for k in range(1, fsdp)]
    near = [lax.rem(lane + k, half) for k in range(1, half)]
    others = [lax.rem(group + k, groups) for k in range(1, groups)]
    partner = lax.rem(me + half, fsdp)

    def load(t):
        e, s = (low + t) // steps, lax.rem(low + t, steps)
        span = pl.ds(pl.multiple_of(s * rows, 8), rows)
        a, b = lax.rem(t, ring), lax.rem(t, wide)
        return (
            pltpu.make_async_copy(master.at[e, :, span, :], held.at[a], master_sem.at[a]),
            pltpu.make_async_copy(second.at[e, :, span, :], narrow.at[b], second_sem.at[b]),
        )

    for t in range(FETCH):
        for copy in load(t):
            copy.start()
    small = ()
    if first:
        small = (pltpu.make_async_copy(router, router_in, small_sem.at[0]),
                 pltpu.make_async_copy(gain, gain_in, small_sem.at[1]))
    for copy in small:
        copy.start()

    barrier = pltpu.get_barrier_semaphore()
    for p in peers:
        pl.semaphore_signal(barrier, inc=1, device_id={"fsdp": p}, device_id_type=MESH)
    if first:
        for g in others:
            pl.semaphore_signal(barrier, inc=1, device_id={"ep": g}, device_id_type=MESH)

    def remote(source, target, send, recv, p):
        return pltpu.make_async_remote_copy(
            source, target, send, recv, device_id={"fsdp": p}, device_id_type=MESH)

    def sums(t):
        for copy in load(t):
            copy.wait()
        a, b = lax.rem(t, ring), lax.rem(t, wide)

        def body(j, _):
            for s in range(2):
                d = s * half + j
                x = held[a, d] + narrow[b, d].astype(jnp.float32)
                held[a, d] = x
                x = x * x
                acc = x[:, :LANES]
                for c in range(LANES, width, LANES):
                    acc = acc + x[:, c:c + LANES]
                if rows < LANES:
                    acc = jnp.concatenate([acc, jnp.zeros((LANES - rows, LANES), jnp.float32)], axis=0)
                part[t, j, pl.ds(s, 1), :] = jnp.sum(acc.T, axis=0, keepdims=True)
            return 0

        lax.fori_loop(0, half, body, 0)

        @pl.when(t + FETCH < chunks)
        def _():
            for copy in load(t + FETCH):
                copy.start()

    def send_whole(t):
        whole[t, me] = part[t]
        for p in peers:
            remote(part.at[t], whole.at[t, me], whole_send.at[t], whole_recv.at[t], p).start()

    def send_near(t):
        gathered[t, lane] = part[t, lane]
        for q in near:
            remote(part.at[t, q], gathered.at[t, lane], near_send.at[t], near_recv.at[t], side * half + q).start()

    def many(ref, t, count, sem):
        block = ref.at[t, pl.ds(0, count)]
        return pltpu.make_async_copy(block, block, sem)

    def put_scale(t, scale):
        scales[t] = jnp.where(side == 0, scale[0:1], scale[1:2])

    def send_far(t):
        many(gathered, t, half - 1, near_recv.at[t]).wait()
        cross[t, side] = jnp.sum(gathered[t], axis=0)
        remote(cross.at[t, side], cross.at[t, side], far_send.at[t], far_recv.at[t], partner).start()

    def send_back(t):
        many(cross, t, 1, far_recv.at[t]).wait()
        scale = jnp.sqrt(cross[t, 0] + cross[t, 1])
        put_scale(t, scale)
        inverse[t, lane] = 1.0 / scale
        for q in near:
            remote(inverse.at[t, lane], inverse.at[t, lane], back_send.at[t], back_recv.at[t], side * half + q).start()

    def take_whole(t):
        many(whole, t, fsdp - 1, whole_recv.at[t]).wait()
        total = whole[t, 0]
        for k in range(1, fsdp):
            total = total + whole[t, k]
        scale = jnp.sqrt(total)
        inverse[t] = 1.0 / scale
        gathered[0] = scale
        put_scale(t, gathered[0, lane])
        many(whole, t, fsdp - 1, whole_send.at[t]).wait()

    def take_back(t):
        many(inverse, t, half - 1, back_recv.at[t]).wait()
        many(gathered, t, half - 1, near_send.at[t]).wait()
        many(cross, t, 1, far_send.at[t]).wait()
        many(inverse, t, half - 1, back_send.at[t]).wait()

    def drain(t):
        many(sent, lax.rem(t, SLOTS), fsdp - 1, block_send.at[lax.rem(t, SLOTS)]).wait()

    def norm(t):
        @pl.when(t >= SLOTS)
        def _():
            drain(t - SLOTS)

        a, out = lax.rem(t, ring), lax.rem(t, SLOTS)
        mine = pl.ds(pl.multiple_of(me * width, LANES), width)
        place = final.at[t, :, mine]

        def block(d):
            row = inverse[t, lax.rem(d, half), pl.ds(d // half, 1), :]
            factor = jnp.broadcast_to(row, (LANES, LANES)).T[:rows]
            for c in range(0, width, LANES):
                sent[out, d, :, c:c + LANES] = (held[a, d, :, c:c + LANES] * factor).astype(jnp.bfloat16)

        def push(d):
            remote(sent.at[out, d], place, block_send.at[out], block_recv.at[me], d).start()

        def body(k, _):
            block(lax.rem(me + k, fsdp))

            @pl.when(k > 1)
            def _():
                push(lax.rem(me + k - 1, fsdp))

            return 0

        lax.fori_loop(1, fsdp, body, 0)
        block(me)
        push(lax.rem(me + fsdp - 1, fsdp))
        final[t, :, mine] = sent[out, me]

    if first:
        sums(0)
        pl.semaphore_wait(barrier, len(peers) + len(others))
    else:
        pl.semaphore_wait(barrier, len(peers))

    def start(t, _):
        @pl.when(t > 0)
        def _():
            sums(t)

        send_whole(t)
        return 0

    if first:
        lax.fori_loop(0, first, start, 0)
        for copy in small:
            copy.wait()
        own = (router_in[...] * gain_in[...]).astype(jnp.bfloat16)
        router_part[...] = own
        routers[group, me] = own
        for p in peers:
            remote(router_part, routers.at[group, me], router_send.at[0], router_recv.at[0], p).start()

    def step(u, _):
        @pl.when(u < chunks)
        def _():
            sums(u)
            send_near(u)

        t = u - AHEAD

        @pl.when((t >= first) & (t < chunks))
        def _():
            send_far(t)

        v = u - 2 * AHEAD

        @pl.when((v >= first) & (v < chunks))
        def _():
            send_back(v)

        w = u - 3 * AHEAD

        if first:
            @pl.when(w < first)
            def _():
                take_whole(w)

        @pl.when(w >= first)
        def _():
            take_back(w)

        @pl.when(w >= 0)
        def _():
            norm(w)

        return 0

    lax.fori_loop(first, chunks + 3 * AHEAD, step, 0)

    if first:
        seven = routers.at[group, pl.ds(0, fsdp - 1)]
        pltpu.make_async_copy(seven, seven, router_send.at[0]).wait()
        pltpu.make_async_copy(seven, seven, router_recv.at[0]).wait()
        for g in others:
            pltpu.make_async_remote_copy(
                routers.at[group], routers.at[group], router_send.at[1], router_recv.at[1],
                device_id={"ep": g}, device_id_type=MESH).start()
        three = routers.at[pl.ds(0, groups - 1)]
        pltpu.make_async_copy(three, three, router_send.at[1]).wait()
        pltpu.make_async_copy(three, three, router_recv.at[1]).wait()

    def last(t, _):
        drain(t)
        return 0

    lax.fori_loop(chunks - SLOTS, chunks, last, 0)
    for c, (start_at, end_at) in enumerate(spans):
        @pl.when(core == c)
        def _(count=end_at - start_at):
            for p in peers:
                column = final.at[pl.ds(0, count), :, pl.ds(pl.multiple_of(p * width, LANES), width)]
                pltpu.make_async_copy(column, column, block_recv.at[p]).wait()


def write_first(cuts, steps, final_in, routers_in, final, router, router_part, sems):
    groups, fsdp, columns, width = routers_in.shape
    core = lax.rem(lax.axis_index("ep"), 2)
    for g in range(groups):
        for d in range(fsdp):
            router_part[g * columns:(g + 1) * columns, d * width:(d + 1) * width] = routers_in[g, d]
    rest = pltpu.make_async_copy(router_part, router, sems.at[0])
    rest.start()
    for c, cut in enumerate(cuts):
        @pl.when(core == c)
        def _(cut=cut):
            ends = list(range(0, cut, steps)) + [cut]
            copies = []
            for k, (a, b) in enumerate(zip(ends, ends[1:])):
                span = pl.ds(a, b - a)
                copies.append(pltpu.make_async_copy(final_in.at[span], final.at[span], sems.at[k + 1]))
            for copy in copies:
                copy.start()
            for copy in copies:
                copy.wait()
    rest.wait()


def write_second(cuts, total, steps, _, late_in, scales_in, late_scales_in, final, scale, scale_part, sems):
    rows = final.shape[1]
    core = lax.rem(lax.axis_index("ep"), 2)
    for c, cut in enumerate(cuts):
        @pl.when(core == c)
        def _(cut=cut):
            big = pltpu.make_async_copy(late_in.at[pl.ds(0, total - cut)], final.at[pl.ds(cut, total - cut)], sems.at[0])
            big.start()
            for e in range(total // steps):
                parts = []
                for t in range(e * steps, (e + 1) * steps):
                    row = scales_in[t] if t < cut else late_scales_in[t - cut]
                    parts.append(row[:, :rows])
                scale_part[e:e + 1, :] = jnp.concatenate(parts, axis=1)
            small = pltpu.make_async_copy(scale_part, scale, sems.at[1])
            small.start()
            big.wait()
            small.wait()


def solution(mesh):
    groups, fsdp = mesh.shape["ep"], mesh.shape["fsdp"]

    def step(master, second, router, gain):
        experts, height, width = master.shape
        own = height // fsdp
        rows = largest_divisor(own, LANES, 8)
        steps = own // rows
        chunks, half = experts * steps, fsdp // 2
        ring, wide = 3 * AHEAD + FETCH + 1, FETCH + 1
        columns = router.shape[1]
        cuts = [chunks - max(chunks // late, SLOTS) for late in LATE]
        hbm = pl.BlockSpec(memory_space=pltpu.HBM)
        inside = pl.BlockSpec(memory_space=pltpu.VMEM)
        dma = pltpu.SemaphoreType.DMA
        dims = (groups, fsdp, steps, rows, width, ring, wide)

        def scratch(count):
            table = (count, half, 2, LANES)
            return [
                pltpu.VMEM((ring, fsdp, rows, width), jnp.float32),
                pltpu.VMEM((wide, fsdp, rows, width), jnp.bfloat16),
                pltpu.VMEM(table, jnp.float32),
                pltpu.VMEM(table, jnp.float32),
                pltpu.VMEM((count, 2, 2, LANES), jnp.float32),
                pltpu.VMEM(table, jnp.float32),
                pltpu.VMEM((SLOTS, fsdp, rows, width), jnp.bfloat16),
                dma((ring,)), dma((wide,)),
                dma((count,)), dma((count,)), dma((count,)), dma((count,)), dma((count,)), dma((count,)),
                dma((SLOTS,)), dma((fsdp,)),
            ]

        def grant(mebibytes, ident=None):
            if ident is None:
                return pltpu.CompilerParams(vmem_limit_bytes=mebibytes * 2**20)
            return pltpu.CompilerParams(
                collective_id=ident, has_side_effects=True, vmem_limit_bytes=mebibytes * 2**20)

        whole = jax.ShapeDtypeStruct((chunks, rows, fsdp * width), jnp.bfloat16)
        master = master.reshape(experts, fsdp, own, width)
        second = second.reshape(experts, fsdp, own, width)
        most, first = max(cuts), 3 * AHEAD
        early, scales, routers = pl.pallas_call(
            functools.partial(exchange, dims, [(0, cut) for cut in cuts], first),
            out_shape=(
                pltpu.VMEM((most, rows, fsdp * width), jnp.bfloat16),
                pltpu.VMEM((most, 1, LANES), jnp.float32),
                pltpu.VMEM((groups, fsdp, columns, width), jnp.bfloat16),
            ),
            in_specs=[hbm, hbm, hbm, hbm],
            out_specs=(inside, inside, inside),
            scratch_shapes=[
                pltpu.VMEM((columns, width), jnp.float32),
                pltpu.VMEM((1, width), jnp.float32),
                pltpu.VMEM((columns, width), jnp.bfloat16),
                pltpu.VMEM((first, fsdp, half, 2, LANES), jnp.float32),
                dma((2,)), dma((first,)), dma((first,)), dma((2,)), dma((2,)),
            ] + scratch(most),
            compiler_params=grant(28, 0),
            name="exchange_early",
        )(
            master,
            second,
            pltpu.with_memory_space_constraint(router.T, pltpu.HBM),
            pltpu.with_memory_space_constraint(gain[None, :], pltpu.HBM),
        )
        final, router = pl.pallas_call(
            functools.partial(write_first, cuts, steps),
            out_shape=(whole, jax.ShapeDtypeStruct((groups * columns, fsdp * width), jnp.bfloat16)),
            in_specs=[inside, inside],
            out_specs=(hbm, hbm),
            scratch_shapes=[
                pltpu.VMEM((groups * columns, fsdp * width), jnp.bfloat16),
                dma((experts + 2,)),
            ],
            compiler_params=grant(2),
            name="write_early",
        )(early, routers)
        most = chunks - min(cuts)
        late, late_scales = pl.pallas_call(
            functools.partial(exchange, dims, [(cut, chunks) for cut in cuts], 0),
            out_shape=(
                pltpu.VMEM((most, rows, fsdp * width), jnp.bfloat16),
                pltpu.VMEM((most, 1, LANES), jnp.float32),
            ),
            in_specs=[hbm, hbm, hbm],
            out_specs=(inside, inside),
            scratch_shapes=scratch(most),
            compiler_params=grant(28, 1),
            name="exchange_late",
        )(master, second, pltpu.with_memory_space_constraint(router, pltpu.HBM))
        final, scale = pl.pallas_call(
            functools.partial(write_second, cuts, chunks, steps),
            out_shape=(whole, jax.ShapeDtypeStruct((experts, own), jnp.float32)),
            in_specs=[hbm, inside, inside, inside],
            out_specs=(hbm, hbm),
            scratch_shapes=[pltpu.VMEM((experts, own), jnp.float32), dma((2,))],
            input_output_aliases={0: 0},
            compiler_params=grant(2),
            name="write_late",
        )(final, late, scales, late_scales)
        return final.reshape(experts, own, fsdp * width), scale, router.T

    return jax.shard_map(
        step,
        mesh=mesh,
        in_specs=(P("ep", None, "fsdp"), P("ep", None, "fsdp"), P("fsdp", "ep"), P("fsdp")),
        out_specs=(P("ep", "fsdp", None), P("ep", "fsdp"), P()),
        check_vma=False,
    )
```

time: 586 us -> 581 us (level); the launches traced: 584 us -> 570 us
  Pallas kernels: 584 us -> 569 us
    pallas_call x2 -> x4, Pallas kernels: 584 us -> 569 us  [the longest x1 429 us: step(): pl.pallas_call(functools.partial(exchange, dims, [(0, cut) for cut in cut...]
where the time goes in v2:
time: 581 us; the launch traced here: 570 us
  Pallas kernels  569 us (98%)
    pallas_call x1, Pallas kernels, step(): pl.pallas_call(functools.partial(exchange, dims, [(0, cut) for cut in cut...  429 us
    pallas_call x1, Pallas kernels, step(): pl.pallas_call(functools.partial(exchange, dims, [(cut, chunks) for cut i...  130 us

profile of v2, /device:TPU:0, one launch (start us, length us, event | category | flops | bytes accessed | tf_op | source)
XLA Modules:
  0.0 569.9 jit_solution(16003288006129573691)
XLA Ops:
  0.6 429.2 %exchange_early.1 = (bf16[32,80,4096]{2,1,0:T(8,128)(2,1)S(1)}, f32[32,1,128]{2,1,0:T(1,128)S(1)}, bf16[4,8,4,512]{3,2,1,0:T(4,128)(2,1)S(1)}) custom-call(f32[4,8,800,512]{3,2,1,0:T(8,128)} %bitcast.6, bf16[4,8,800,512]{3,2,1,0:T(8,128)(2,1)} %bitcast.8, f32[4,512]{1,0:T(4,128)} %bitcast.12, f32[1,512]{1,0:T(1,128)} %bitcast.13), custom_call_target="tpu_custom_call" | custom-call | tf_op jit(solution)/shard_map/exchange_early/pallas_call | solution.py:351
  429.8 7.3 %write_early.1 = (bf16[40,80,4096]{2,1,0:T(8,128)(2,1)}, bf16[16,4096]{1,0:T(8,128)(2,1)}) custom-call(bf16[32,80,4096]{2,1,0:T(8,128)(2,1)S(1)} %get-tuple-element.12.final_in, bf16[4,8,4,512]{3,2,1,0:T(4,128)(2,1)S(1)} %get-tuple-element.13.routers_in), custom_call_target="tpu_custom_call" | custom-call | tf_op jit(solution)/shard_map/write_early/pallas_call | solution.py:375
  437.1 130.4 %exchange_late.1 = (bf16[13,80,4096]{2,1,0:T(8,128)(2,1)S(1)}, f32[13,1,128]{2,1,0:T(1,128)S(1)}) custom-call(f32[4,8,800,512]{3,2,1,0:T(8,128)} %bitcast.7, bf16[4,8,800,512]{3,2,1,0:T(8,128)(2,1)} %bitcast.9, bf16[16,4096]{1,0:T(8,128)(2,1)} %get-tuple-element.15.refs_2_), custom_call_target="tpu_custom_call" | custom-call | tf_op jit(solution)/shard_map/exchange_late/pallas_call | solution.py:388
  567.5 2.4 write_late.1

commit v3 on v2

--- a/solution.py
+++ b/solution.py
@@ -12,7 +12,7 @@
 AHEAD = 2
 SLOTS = 4
 FETCH = 3
-LATE = (5, 3)
+LATE = (10, 4)
 
 
 def largest_divisor(size, limit, step):
@@ -201,44 +201,7 @@
         for p in peers:
             remote(router_part, routers.at[group, me], router_send.at[0], router_recv.at[0], p).start()
 
-    def step(u, _):
-        @pl.when(u < chunks)
-        def _():
-            sums(u)
-            send_near(u)
-
-        t = u - AHEAD
-
-        @pl.when((t >= first) & (t < chunks))
-        def _():
-            send_far(t)
-
-        v = u - 2 * AHEAD
-
-        @pl.when((v >= first) & (v < chunks))
-        def _():
-            send_back(v)
-
-        w = u - 3 * AHEAD
-
-        if first:
-            @pl.when(w < first)
-            def _():
-                take_whole(w)
-
-        @pl.when(w >= first)
-        def _():
-            take_back(w)
-
-        @pl.when(w >= 0)
-        def _():
-            norm(w)
-
-        return 0
-
-    lax.fori_loop(first, chunks + 3 * AHEAD, step, 0)
-
-    if first:
+    def send_router():
         seven = routers.at[group, pl.ds(0, fsdp - 1)]
         pltpu.make_async_copy(seven, seven, router_send.at[0]).wait()
         pltpu.make_async_copy(seven, seven, router_recv.at[0]).wait()
@@ -246,6 +209,50 @@
             pltpu.make_async_remote_copy(
                 routers.at[group], routers.at[group], router_send.at[1], router_recv.at[1],
                 device_id={"ep": g}, device_id_type=MESH).start()
+
+    def step(u, _):
+        @pl.when(u < chunks)
+        def _():
+            sums(u)
+            send_near(u)
+
+        t = u - AHEAD
+
+        @pl.when((t >= first) & (t < chunks))
+        def _():
+            send_far(t)
+
+        v = u - 2 * AHEAD
+
+        @pl.when((v >= first) & (v < chunks))
+        def _():
+            send_back(v)
+
+        w = u - 3 * AHEAD
+
+        if first:
+            @pl.when(w < first)
+            def _():
+                take_whole(w)
+
+        @pl.when(w >= first)
+        def _():
+            take_back(w)
+
+        @pl.when(w >= 0)
+        def _():
+            norm(w)
+
+        if first:
+            @pl.when(w == SLOTS)
+            def _():
+                send_router()
+
+        return 0
+
+    lax.fori_loop(first, chunks + 3 * AHEAD, step, 0)
+
+    if first:
         three = routers.at[pl.ds(0, groups - 1)]
         pltpu.make_async_copy(three, three, router_send.at[1]).wait()
         pltpu.make_async_copy(three, three, router_recv.at[1]).wait()

time: 581 us -> 578 us (level); the launches traced: 570 us -> 578 us
  Pallas kernels: 569 us -> 578 us
    pallas_call x1, Pallas kernels: 429 us -> 501 us  [step(): pl.pallas_call(functools.partial(exchange, dims, [(0, cut) for cut in cut...]
    pallas_call x1, Pallas kernels: 130 us -> 67.2 us  [step(): pl.pallas_call(functools.partial(exchange, dims, [(cut, chunks) for cut i...]
where the time goes in v3:
time: 578 us
  Pallas kernels  578 us (100%)
    pallas_call x1, Pallas kernels, step(): pl.pallas_call(functools.partial(exchange, dims, [(0, cut) for cut in cut...  501 us
    pallas_call x1, Pallas kernels, step(): pl.pallas_call(functools.partial(exchange, dims, [(cut, chunks) for cut i...  67.2 us

profile of v3, /device:TPU:0, one launch (start us, length us, event | category | flops | bytes accessed | tf_op | source)
XLA Modules:
  0.0 578.3 jit_solution(16004427296151265791)
XLA Ops:
  0.6 500.8 %exchange_early.1 = (bf16[36,80,4096]{2,1,0:T(8,128)(2,1)S(1)}, f32[36,1,128]{2,1,0:T(1,128)S(1)}, bf16[4,8,4,512]{3,2,1,0:T(4,128)(2,1)S(1)}) custom-call(f32[4,8,800,512]{3,2,1,0:T(8,128)} %bitcast.6, bf16[4,8,800,512]{3,2,1,0:T(8,128)(2,1)} %bitcast.8, f32[4,512]{1,0:T(4,128)} %bitcast.12, f32[1,512]{1,0:T(1,128)} %bitcast.13), custom_call_target="tpu_custom_call" | custom-call | tf_op jit(solution)/shard_map/exchange_early/pallas_call | solution.py:358
  501.4 8.2 %write_early.1 = (bf16[40,80,4096]{2,1,0:T(8,128)(2,1)}, bf16[16,4096]{1,0:T(8,128)(2,1)}) custom-call(bf16[36,80,4096]{2,1,0:T(8,128)(2,1)S(1)} %get-tuple-element.12.final_in, bf16[4,8,4,512]{3,2,1,0:T(4,128)(2,1)S(1)} %get-tuple-element.13.routers_in), custom_call_target="tpu_custom_call" | custom-call | tf_op jit(solution)/shard_map/write_early/pallas_call | solution.py:382
  509.6 67.2 %exchange_late.1 = (bf16[10,80,4096]{2,1,0:T(8,128)(2,1)S(1)}, f32[10,1,128]{2,1,0:T(1,128)S(1)}) custom-call(f32[4,8,800,512]{3,2,1,0:T(8,128)} %bitcast.7, bf16[4,8,800,512]{3,2,1,0:T(8,128)(2,1)} %bitcast.9, bf16[16,4096]{1,0:T(8,128)(2,1)} %get-tuple-element.15.refs_2_), custom_call_target="tpu_custom_call" | custom-call | tf_op jit(solution)/shard_map/exchange_late/pallas_call | solution.py:395
  576.8 1.6 write_late.1

commit v4 on v3

--- a/solution.py
+++ b/solution.py
@@ -211,23 +211,6 @@
                 device_id={"ep": g}, device_id_type=MESH).start()
 
     def step(u, _):
-        @pl.when(u < chunks)
-        def _():
-            sums(u)
-            send_near(u)
-
-        t = u - AHEAD
-
-        @pl.when((t >= first) & (t < chunks))
-        def _():
-            send_far(t)
-
-        v = u - 2 * AHEAD
-
-        @pl.when((v >= first) & (v < chunks))
-        def _():
-            send_back(v)
-
         w = u - 3 * AHEAD
 
         if first:
@@ -242,6 +225,23 @@
         @pl.when(w >= 0)
         def _():
             norm(w)
+
+        @pl.when(u < chunks)
+        def _():
+            sums(u)
+            send_near(u)
+
+        t = u - AHEAD
+
+        @pl.when((t >= first) & (t < chunks))
+        def _():
+            send_far(t)
+
+        v = u - 2 * AHEAD
+
+        @pl.when((v >= first) & (v < chunks))
+        def _():
+            send_back(v)
 
         if first:
             @pl.when(w == SLOTS)

time: 578 us -> 578 us (level)
  no operation moved by 1% of the time
where the time goes in v4:
time: 578 us; the launch traced here: 577 us
  Pallas kernels  576 us (100%)
    pallas_call x1, Pallas kernels, step(): pl.pallas_call(functools.partial(exchange, dims, [(0, cut) for cut in cut...  502 us
    pallas_call x1, Pallas kernels, step(): pl.pallas_call(functools.partial(exchange, dims, [(cut, chunks) for cut i...  64.6 us

profile of v4, /device:TPU:0, one launch (start us, length us, event | category | flops | bytes accessed | tf_op | source)
XLA Modules:
  0.0 576.5 jit_solution(15233236611591456292)
XLA Ops:
  0.6 501.6 %exchange_early.1 = (bf16[36,80,4096]{2,1,0:T(8,128)(2,1)S(1)}, f32[36,1,128]{2,1,0:T(1,128)S(1)}, bf16[4,8,4,512]{3,2,1,0:T(4,128)(2,1)S(1)}) custom-call(f32[4,8,800,512]{3,2,1,0:T(8,128)} %bitcast.6, bf16[4,8,800,512]{3,2,1,0:T(8,128)(2,1)} %bitcast.8, f32[4,512]{1,0:T(4,128)} %bitcast.12, f32[1,512]{1,0:T(1,128)} %bitcast.13), custom_call_target="tpu_custom_call" | custom-call | tf_op jit(solution)/shard_map/exchange_early/pallas_call | solution.py:358
  502.2 8.2 %write_early.1 = (bf16[40,80,4096]{2,1,0:T(8,128)(2,1)}, bf16[16,4096]{1,0:T(8,128)(2,1)}) custom-call(bf16[36,80,4096]{2,1,0:T(8,128)(2,1)S(1)} %get-tuple-element.12.final_in, bf16[4,8,4,512]{3,2,1,0:T(4,128)(2,1)S(1)} %get-tuple-element.13.routers_in), custom_call_target="tpu_custom_call" | custom-call | tf_op jit(solution)/shard_map/write_early/pallas_call | solution.py:382
  510.4 64.6 %exchange_late.1 = (bf16[10,80,4096]{2,1,0:T(8,128)(2,1)S(1)}, f32[10,1,128]{2,1,0:T(1,128)S(1)}) custom-call(f32[4,8,800,512]{3,2,1,0:T(8,128)} %bitcast.7, bf16[4,8,800,512]{3,2,1,0:T(8,128)(2,1)} %bitcast.9, bf16[16,4096]{1,0:T(8,128)(2,1)} %get-tuple-element.15.refs_2_), custom_call_target="tpu_custom_call" | custom-call | tf_op jit(solution)/shard_map/exchange_late/pallas_call | solution.py:395
  575.0 1.6 write_late.1
